TPU v7x, 32 devices: a whole 2x2x4 slice. The times are simulated.
32 devices in a mesh: seq: 8 (over z, x), head: 4 (over y, core).
Axes of the slice: x: 2, y: 2, z: 4, core: 2. Of those that a mesh axis runs over, the one named last changes fastest.
Arguments:
- patches: bfloat16 [32768, 768], P('seq'), may hold values from -6 to 6
- slot_image: int32 [128], P('seq'), may hold values from -1 to 63, as said below
- slot_dest: int32 [128], P('seq'), may hold values from -1 to 63, as said below
- enc_gain: float32 [768], replicated, may hold values from 0.1 to 1.9
- w_qkv: bfloat16 [3, 768, 768], P(None, None, 'head'), may hold values from -1.2 to 1.2
- w_out: bfloat16 [768, 768], P('head'), may hold values from -0.21875 to 0.21875
- fast_gain: float32 [768], replicated, may hold values from 0.1 to 1.9
- w_fast: bfloat16 [3, 768, 768], P(None, None, 'head'), may hold values from -0.21875 to 0.21875
- w_rate: bfloat16 [768, 4], P(None, 'head'), may hold values from -0.21875 to 0.21875
- fast_gate_up: float32 [4, 2, 192, 384], P('head'), may hold values from -0.4375 to 0.4375
- fast_down: float32 [4, 384, 192], P('head'), may hold values from -0.3125 to 0.3125
Outputs:
- view_out: bfloat16 [16384, 768], P('seq', 'head')
Inputs may be any that keep to these rules, and one draw needn't show every extreme that they name: slot_dest gives for each slot the view-order block that its block becomes, or -1 for an empty slot; every view-order block is named by exactly one slot. Slots 2i and 2i + 1 of one seq index are both empty or name view blocks 2m and 2m + 1. The slots of one seq index name at most 2 blocks of any one view shard (blocks s * 8 to (s + 1) * 8 - 1), and some seq index uses all of its slots. slot_image is -1 exactly where slot_dest is -1; an image is one block or the two blocks of a slot pair, and different images have different ids.
All inputs are finite; a program needn't handle non-finite values.
Results may differ from a plain program's by a relative error of at most 0.035.
Values may be sent and summed in bfloat16 or wider, within the bound.
A program may use at most 128 MiB of HBM per device.

v0:
```python
import jax
import jax.numpy as jnp
from jax import lax
from jax.sharding import PartitionSpec as P

HDIM = 64
BLK = 256
BLK_DEV = 8
EPSILON = 1e-06
RATE_SCALE = 0.1


def norm_rows(values, gain_vector):
    widened = values.astype(jnp.float32)
    factor = lax.rsqrt(jnp.mean(widened * widened, axis=-1, keepdims=True) + EPSILON)
    return (widened * factor * gain_vector).astype(jnp.bfloat16)


def attend_pair(pieces):
    query_rows, key_rows, value_rows, token_ids = pieces
    token_count = query_rows.shape[0]
    heads_here = query_rows.shape[1] // HDIM
    q_heads = query_rows.reshape(token_count, heads_here, HDIM)
    k_heads = key_rows.reshape(token_count, heads_here, HDIM)
    v_heads = value_rows.reshape(token_count, heads_here, HDIM)
    scores = jnp.einsum(
        "qhe,khe->hqk", q_heads, k_heads, preferred_element_type=jnp.float32
    ) * HDIM ** (-0.5)
    allowed = token_ids[:, None] == token_ids[None, :]
    scores = jnp.where(allowed[None], scores, -1e30)
    top_score = jnp.max(scores, axis=-1, keepdims=True)
    exp_scores = jnp.exp(scores - top_score)
    weights = (exp_scores / jnp.sum(exp_scores, axis=-1, keepdims=True)).astype(jnp.bfloat16)
    mixed_heads = jnp.einsum("hqk,khe->qhe", weights, v_heads, preferred_element_type=jnp.float32)
    return mixed_heads.astype(jnp.bfloat16).reshape(token_count, heads_here * HDIM)


def encode_blocks(full_rows, block_ids, enc_gain, w_qkv):
    normed = norm_rows(full_rows, enc_gain)
    query_rows = jnp.dot(normed, w_qkv[0], preferred_element_type=jnp.float32).astype(jnp.bfloat16)
    key_rows = jnp.dot(normed, w_qkv[1], preferred_element_type=jnp.float32).astype(jnp.bfloat16)
    value_rows = jnp.dot(normed, w_qkv[2], preferred_element_type=jnp.float32).astype(jnp.bfloat16)
    columns = query_rows.shape[1]
    span = 2 * BLK
    pair_count = full_rows.shape[0] // span
    token_ids = jnp.repeat(block_ids, BLK, total_repeat_length=pair_count * span).reshape(
        pair_count, span
    )
    attended = lax.map(
        attend_pair,
        (
            query_rows.reshape(pair_count, span, columns),
            key_rows.reshape(pair_count, span, columns),
            value_rows.reshape(pair_count, span, columns),
            token_ids,
        ),
    )
    return attended.reshape(pair_count * span, columns)


def route_matrix(destinations, seq_count, room):
    slot_count = destinations.shape[0]
    target_seq = jnp.where(destinations >= 0, destinations // BLK_DEV, -1)
    position = jnp.arange(slot_count)
    earlier = position[None, :] < position[:, None]
    same_target = (target_seq[None, :] == target_seq[:, None]) & earlier
    ranking = jnp.sum(same_target.astype(jnp.int32), axis=1)
    bucket = jnp.where(destinations >= 0, target_seq * room + ranking, -1)
    return bucket[None, :] == jnp.arange(seq_count * room)[:, None]


def pack_rows(selection, payload):
    return jnp.dot(
        selection.astype(jnp.bfloat16), payload, preferred_element_type=jnp.float32
    ).astype(jnp.bfloat16)


def pack_index(selection, indices):
    return jnp.sum(jnp.where(selection, indices[None, :] + 1, 0), axis=1).astype(jnp.int32) - 1


def place_matrix(arrived, seq_index):
    local_block = arrived - seq_index * BLK_DEV
    return (local_block[None, :] == jnp.arange(BLK_DEV)[:, None]) & (arrived >= 0)[None, :]


def renorm(updated, initial):
    target_norm = jnp.sqrt(jnp.sum(initial * initial, axis=1, keepdims=True))
    return (
        updated
        * target_norm
        * lax.rsqrt(jnp.sum(updated * updated, axis=1, keepdims=True) + EPSILON)
    )


def on_device(
    patches,
    slot_image,
    slot_dest,
    enc_gain,
    w_qkv,
    w_out,
    fast_gain,
    w_fast,
    w_rate,
    fast_gate_up,
    fast_down,
):
    seq_count = lax.axis_size("seq")
    seq_index = lax.axis_index("seq")
    head_index = lax.axis_index("head")
    width = w_out.shape[0]
    slot_count = slot_dest.shape[0]
    room = 2 * ((BLK_DEV + seq_count - 1) // seq_count)
    patch_blocks = patches.reshape(slot_count, BLK, patches.shape[1])
    own_columns = lax.dynamic_slice_in_dim(patch_blocks, head_index * width, width, 2).reshape(
        slot_count, BLK * width
    )
    selection = route_matrix(slot_dest, seq_count, room)
    sent_dest = pack_index(selection, slot_dest)
    got_own, arrived, got_ids = (
        lax.all_to_all(
            pack_rows(selection, own_columns), "seq", split_axis=0, concat_axis=0, tiled=True
        ),
        lax.all_to_all(sent_dest, "seq", split_axis=0, concat_axis=0, tiled=True),
        lax.all_to_all(
            pack_index(selection, slot_image), "seq", split_axis=0, concat_axis=0, tiled=True
        ),
    )
    placing = place_matrix(arrived, seq_index)
    view_own = pack_rows(placing, got_own)
    view_ids = pack_index(placing, got_ids)
    whole_rows = lax.all_gather(view_own.reshape(BLK_DEV * BLK, width), "head", axis=1, tiled=True)
    view_attn = encode_blocks(whole_rows, view_ids, enc_gain, w_qkv)
    partial_value = jnp.dot(view_attn, w_out, preferred_element_type=jnp.float32)
    head_mixed = lax.psum_scatter(
        partial_value.astype(jnp.bfloat16), "head", scatter_dimension=1, tiled=True
    ).astype(jnp.float32)
    embedded = (head_mixed + view_own.reshape(BLK_DEV * BLK, width).astype(jnp.float32)).astype(
        jnp.bfloat16
    )
    full_embedded = lax.all_gather(embedded, "head", axis=1, tiled=True)
    normed_fast = norm_rows(full_embedded, fast_gain)
    fast_query = jnp.dot(normed_fast, w_fast[0], preferred_element_type=jnp.float32).astype(
        jnp.bfloat16
    )
    fast_key = jnp.dot(normed_fast, w_fast[1], preferred_element_type=jnp.float32).astype(
        jnp.bfloat16
    )
    fast_value = jnp.dot(normed_fast, w_fast[2], preferred_element_type=jnp.float32).astype(
        jnp.bfloat16
    )
    token_total = embedded.shape[0] * seq_count
    rates = (
        RATE_SCALE
        * jax.nn.softplus(jnp.dot(normed_fast, w_rate, preferred_element_type=jnp.float32))
        * token_total ** (-0.5)
    )
    gate_init = fast_gate_up[0, 0]
    up_init = fast_gate_up[0, 1]
    down_init = fast_down[0]
    gate_half = gate_init.astype(jnp.bfloat16)
    up_half = up_init.astype(jnp.bfloat16)
    down_half = down_init.astype(jnp.bfloat16)
    key_gate = jnp.dot(fast_key, gate_half, preferred_element_type=jnp.float32)
    key_up = jnp.dot(fast_key, up_half, preferred_element_type=jnp.float32)
    hidden_key = (jax.nn.silu(key_gate) * key_up).astype(jnp.bfloat16)
    out_grad = (-rates * fast_value.astype(jnp.float32)).astype(jnp.bfloat16)
    grad_down = jnp.einsum("th,tf->hf", hidden_key, out_grad, preferred_element_type=jnp.float32)
    hidden_grad = jnp.dot(out_grad, down_half.T, preferred_element_type=jnp.float32)
    sigmoid_gate = jax.nn.sigmoid(key_gate)
    gate_grad = (
        hidden_grad * key_up * sigmoid_gate * (1.0 + key_gate * (1.0 - sigmoid_gate))
    ).astype(jnp.bfloat16)
    up_grad = (hidden_grad * jax.nn.silu(key_gate)).astype(jnp.bfloat16)
    grad_gate = jnp.einsum("tf,th->fh", fast_key, gate_grad, preferred_element_type=jnp.float32)
    grad_up = jnp.einsum("tf,th->fh", fast_key, up_grad, preferred_element_type=jnp.float32)
    grad_gate, grad_up, grad_down = (
        lax.psum(grad_gate.astype(jnp.bfloat16), "seq").astype(jnp.float32),
        lax.psum(grad_up.astype(jnp.bfloat16), "seq").astype(jnp.float32),
        lax.psum(grad_down.astype(jnp.bfloat16), "seq").astype(jnp.float32),
    )
    new_gate = renorm(gate_init - grad_gate, gate_init)
    new_up = renorm(up_init - grad_up, up_init)
    new_down = renorm(down_init - grad_down, down_init)
    applied_gate = new_gate.astype(jnp.bfloat16)
    applied_up = new_up.astype(jnp.bfloat16)
    applied_down = new_down.astype(jnp.bfloat16)
    query_gate = jnp.dot(fast_query, applied_gate, preferred_element_type=jnp.float32)
    query_up = jnp.dot(fast_query, applied_up, preferred_element_type=jnp.float32)
    query_hidden = (jax.nn.silu(query_gate) * query_up).astype(jnp.bfloat16)
    fast_out = jnp.dot(query_hidden, applied_down, preferred_element_type=jnp.float32)
    return (embedded.astype(jnp.float32) + fast_out).astype(jnp.bfloat16)


def solution(mesh):
    in_specs = (
        P("seq", None),
        P("seq"),
        P("seq"),
        P(),
        P(None, None, "head"),
        P("head", None),
        P(),
        P(None, None, "head"),
        P(None, "head"),
        P("head", None, None, None),
        P("head", None, None),
    )
    out_specs = P("seq", "head")
    return jax.shard_map(
        on_device, mesh=mesh, in_specs=in_specs, out_specs=out_specs, check_vma=False
    )
```

profile of v0, /device:TPU:0, one launch (start us, length us, event | category | flops | bytes accessed | tf_op | source)
XLA Modules:
  0.0 311.4 jit_solution(212847610619158784)
XLA Ops:
  9.6 7.3 %all-to-all-start = ((s32[8,2,1]{1,2,0:T(1,128)}), s32[8,2,1]{1,2,0:T(1,128)S(1)}, u32[]{:S(2)}, u32[]{:S(2)}) async-start(s32[8,2,1]{1,2,0:T(1,128)} %bitcast.6), calls=%async_computation | async-start | bytes 8192 | tf_op jit(solution)/shard_map/all_to_all | solution.py:125
  16.8 2.9 constant_dynamic-slice_fusion.4
  19.8 3.2 %reshape.274 = bf16[16,49152]{1,0:T(8,128)(2,1)} reshape(bf16[16,256,192]{2,1,0:T(8,128)(2,1)S(1)} %constant_dynamic-slice_fusion.4) | data formatting | bytes 3145728 | tf_op jit(solution)/shard_map/reshape | solution.py:116
  23.0 2.0 convolution_convert_fusion
  24.9 1.9 all_to_all.17
  26.9 6.0 %all-to-all-start.1 = ((bf16[8,2,49152]{2,1,0:T(2,128)(2,1)}), bf16[8,2,49152]{2,1,0:T(2,128)(2,1)S(1)}, u32[]{:S(2)}, u32[]{:S(2)}) async-start(bf16[8,2,49152]{2,1,0:T(2,128)(2,1)} %all_to_all.17), calls=%async_computation.1 | async-start | bytes 3145728 | tf_op jit(solution)/shard_map/all_to_all | solution.py:122
  33.1 36.2 %all-to-all-done.1 = bf16[8,2,49152]{2,1,0:T(2,128)(2,1)S(1)} async-done(((bf16[8,2,49152]{2,1,0:T(2,128)(2,1)}), bf16[8,2,49152]{2,1,0:T(2,128)(2,1)S(1)}, u32[]{:S(2)}, u32[]{:S(2)}) %all-to-all-start.1) | async-done | bytes 1572896 | tf_op jit(solution)/shard_map/all_to_all | solution.py:122
  71.3 2.3 reshape.275
  75.5 3.6 %all-to-all-start.2 = ((s32[8,2,1]{1,2,0:T(1,128)}), s32[8,2,1]{1,2,0:T(1,128)S(1)}, u32[]{:S(2)}, u32[]{:S(2)}) async-start(s32[8,2,1]{1,2,0:T(1,128)} %bitcast.9), calls=%async_computation.2 | async-start | bytes 8192 | tf_op jit(solution)/shard_map/all_to_all | solution.py:126
  79.4 6.3 %all-to-all-done.2 = s32[8,2,1]{1,2,0:T(1,128)S(1)} async-done(((s32[8,2,1]{1,2,0:T(1,128)}), s32[8,2,1]{1,2,0:T(1,128)S(1)}, u32[]{:S(2)}, u32[]{:S(2)}) %all-to-all-start.2) | async-done | bytes 96 | tf_op jit(solution)/shard_map/all_to_all | solution.py:126
  86.6 5.0 %select_select_fusion = s32[2048]{0:T(1024)S(1)} fusion(pred[2048]{0:T(1024)(128)(4,1)S(1)} %copy-done.21, pred[2048]{0:T(1024)(128)(4,1)S(1)} %copy-done.20, pred[2048]{0:T(1024)(128)(4,1)S(1)} %copy-done.19, pred[2048]{0:T(1024)(128)(4,1)S(1)} %copy-done.18, pred[2048]{0:T(1024)(128)(4,1)S(1)} %copy-done.17, pred[2048]{0:T(1024)(128)(4,1)S(1)} %copy-done.16, ...), kind=kLoop, calls=%fused_computation.103 | loop fusion | flops 14336 | bytes 22560 | tf_op jit(solution)/shard_map/jit(_take)/gather | solution.py:46
  91.6 10.7 %all-gather.3.cloned.1.call-done = bf16[2048,768]{0,1:T(8,128)(2,1)} async-done(((bf16[2048,192]{0,1:T(8,128)(2,1)}), bf16[2048,768]{0,1:T(8,128)(2,1)}) %all-gather.3.cloned.1.call-update) | async-done | bytes 3145744 | tf_op jit(solution)/shard_map/all_gather | solution.py:133
  102.3 2.7 fusion.11
  108.6 25.0 %while.11 = (s32[]{:T(128)}, bf16[4,512,192]{1,2,0:T(8,128)(2,1)}, bf16[4,512,192]{1,2,0:T(8,128)(2,1)S(1)}, s32[4,512]{1,0:T(4,128)S(1)}, bf16[4,512,192]{1,2,0...) while((s32[]{:T(128)}, bf16[4,512,192]{1,2,0:T(8,128)(2,1)}, ...), condition=%wide.region_8.9_spmd, body=%wide.region_5.8_spmd.sunk | while | flops 206406144 | bytes 9193573 | solution.py:49
  109.0 3.0 fusion.111
  111.9 2.3 fusion.112
  115.2 3.0 fusion.111
  118.2 2.3 fusion.112
  121.4 3.0 fusion.111
  124.4 2.3 fusion.112
  127.7 3.0 fusion.111
  130.6 2.3 fusion.112
  134.9 2.7 convolution_convert_fusion.2
  137.6 38.0 %reduce-scatter.2.cloned.1.call-done = bf16[2048,192]{0,1:T(8,128)(2,1)} async-done(((bf16[2048,768]{0,1:T(8,128)(2,1)}), bf16[2048,192]{0,1:T(8,128)(2,1)}) %reduce-scatter.2.cloned.1.call-update) | async-done | bytes 786448 | tf_op jit(solution)/shard_map/reduce_scatter | solution.py:136
  175.6 2.3 add_convert_fusion
  178.2 28.4 %all-gather.5.cloned.1.call-done = bf16[2048,768]{0,1:T(8,128)(2,1)} async-done(((bf16[2048,192]{0,1:T(8,128)(2,1)}), bf16[2048,768]{0,1:T(8,128)(2,1)}) %all-gather.5.cloned.1.call-update) | async-done | bytes 3145744 | tf_op jit(solution)/shard_map/all_gather | solution.py:142
  206.6 2.7 fusion.14
  217.3 2.1 fusion.27
  221.2 2.6 convolution_convert_fusion.5
  223.8 70.4 %all-reduce.3.cloned.1.call-done = (bf16[192,384]{1,0:T(8,128)(2,1)}, bf16[192,384]{1,0:T(8,128)(2,1)}, bf16[384,192]{0,1:T(8,128)(2,1)}) async-done(((bf16[192,384]{1,0:T(8,128)(2,1)}, bf16[192,384]{1,0:T(8,128)(2,1)}, bf16[384,192]{0,1:T(8,128)(2,1)}), (bf16[192,384]{1,0:T(8,128)(2,1)}, bf16[192,384]{1,0:T(8,128)(2,1)}, bf16[384,192]{0,1:T(8,128)(2,1)})) %all-reduce.3.cloned.1.call-update) | async-done | bytes 442384 | tf_op jit(solution)/shard_map/psum | solution.py:179
  296.8 3.8 %fusion.45 = f32[2048,384]{1,0:T(8,128)} fusion(bf16[2048,192]{0,1:T(8,128)(2,1)} %convolution_convert_fusion.5, bf16[192,384]{1,0:T(8,128)(2,1)} %get-tuple-element.94, f32[1,2,192,384]{3,2,1,0:T(8,128)} %param.24, f32[192]{0:T(256)S(1)} %add_rsqrt_fusion.4, f32[192]{0:T(256)S(1)} %sqrt.24), kind=kOutput, calls=%fused_computation.89 | convolution fusion | flops 302358528 | bytes 4376064 | tf_op jit(solution)/shard_map/dot_general | solution.py:189
  300.6 4.3 %fusion.18 = bf16[2048,192]{0,1:T(8,128)(2,1)} fusion(bf16[2048,192]{0,1:T(8,128)(2,1)S(1)} %copy-done.6, f32[2048,384]{1,0:T(8,128)} %fusion.45, bf16[2048,192]{0,1:T(8,128)(2,1)S(1)} %copy-done.7, bf16[192,384]{1,0:T(8,128)(2,1)S(1)} %copy-done.11, f32[1,2,192,384]{3,2,1,0:T(8,128)S(1)} %copy-done.4, bf16[384,192]{0,1:T(8,128)(2,1)S(1)} %copy-done.12, ...), kind=kOutput, calls=%fused_computation.39 | convolution fusion | flops 610615296 | bytes 6395904 | tf_op jit(solution)/shard_map/dot_general | solution.py:192
  (126 shorter events, 29.4 us)
Async XLA Ops:
  6.5 128.3 %copy-start = (bf16[192,768]{1,0:T(8,128)(2,1)S(1)}, bf16[192,768]{1,0:T(8,128)(2,1)}, u32[]{:S(2)}) copy-start(bf16[192,768]{1,0:T(8,128)(2,1)} %param.20) | copy-start | bytes 884740
  9.6 17.3 %all-to-all-start = ((s32[8,2,1]{1,2,0:T(1,128)}), s32[8,2,1]{1,2,0:T(1,128)S(1)}, u32[]{:S(2)}, u32[]{:S(2)}) async-start(s32[8,2,1]{1,2,0:T(1,128)} %bitcast.6), calls=%async_computation | async-start | bytes 8192 | tf_op jit(solution)/shard_map/all_to_all | solution.py:125
  26.9 42.4 %all-to-all-start.1 = ((bf16[8,2,49152]{2,1,0:T(2,128)(2,1)}), bf16[8,2,49152]{2,1,0:T(2,128)(2,1)S(1)}, u32[]{:S(2)}, u32[]{:S(2)}) async-start(bf16[8,2,49152]{2,1,0:T(2,128)(2,1)} %all_to_all.17), calls=%async_computation.1 | async-start | bytes 3145728 | tf_op jit(solution)/shard_map/all_to_all | solution.py:122
  32.9 69.4 %all-gather.3.cloned.1.call-start = ((), (), s32[]{:S(2)}) async-start(), calls=%async_computation.4 | async-start | bytes 3932160 | tf_op jit(solution)/shard_map/all_gather | solution.py:133
  69.9 16.6 %copy-start.15 = (pred[2048]{0:T(1024)(128)(4,1)S(1)}, pred[2048]{0:T(1024)(128)(4,1)}, u32[]{:S(2)}) copy-start(pred[2048]{0:T(1024)(128)(4,1)} %constant.200) | copy-start | bytes 6148
  70.0 16.6 %copy-start.16 = (pred[2048]{0:T(1024)(128)(4,1)S(1)}, pred[2048]{0:T(1024)(128)(4,1)}, u32[]{:S(2)}) copy-start(pred[2048]{0:T(1024)(128)(4,1)} %constant.199) | copy-start | bytes 6148
  70.0 16.6 %copy-start.17 = (pred[2048]{0:T(1024)(128)(4,1)S(1)}, pred[2048]{0:T(1024)(128)(4,1)}, u32[]{:S(2)}) copy-start(pred[2048]{0:T(1024)(128)(4,1)} %constant.198) | copy-start | bytes 6148
  70.0 16.6 %copy-start.18 = (pred[2048]{0:T(1024)(128)(4,1)S(1)}, pred[2048]{0:T(1024)(128)(4,1)}, u32[]{:S(2)}) copy-start(pred[2048]{0:T(1024)(128)(4,1)} %constant.197) | copy-start | bytes 6148
  70.0 16.6 %copy-start.19 = (pred[2048]{0:T(1024)(128)(4,1)S(1)}, pred[2048]{0:T(1024)(128)(4,1)}, u32[]{:S(2)}) copy-start(pred[2048]{0:T(1024)(128)(4,1)} %constant.196) | copy-start | bytes 6148
  70.0 16.6 %copy-start.20 = (pred[2048]{0:T(1024)(128)(4,1)S(1)}, pred[2048]{0:T(1024)(128)(4,1)}, u32[]{:S(2)}) copy-start(pred[2048]{0:T(1024)(128)(4,1)} %constant.195) | copy-start | bytes 6148
  70.0 16.6 %copy-start.21 = (pred[2048]{0:T(1024)(128)(4,1)S(1)}, pred[2048]{0:T(1024)(128)(4,1)}, u32[]{:S(2)}) copy-start(pred[2048]{0:T(1024)(128)(4,1)} %constant.194) | copy-start | bytes 6148
  73.6 31.4 %copy-start.22 = (bf16[3,768,192]{1,2,0:T(8,128)(2,1)S(1)}, bf16[3,768,192]{1,2,0:T(8,128)(2,1)}, u32[]{:S(2)}) copy-start(bf16[3,768,192]{1,2,0:T(8,128)(2,1)} %param.19) | copy-start | bytes 2654212
  73.6 31.4 %copy-start.23 = (f32[768]{0:T(1024)S(1)}, f32[768]{0:T(1024)}, u32[]{:S(2)}) copy-start(f32[768]{0:T(1024)} %param.18) | copy-start | bytes 9220
  75.5 10.1 %all-to-all-start.2 = ((s32[8,2,1]{1,2,0:T(1,128)}), s32[8,2,1]{1,2,0:T(1,128)S(1)}, u32[]{:S(2)}, u32[]{:S(2)}) async-start(s32[8,2,1]{1,2,0:T(1,128)} %bitcast.9), calls=%async_computation.2 | async-start | bytes 8192 | tf_op jit(solution)/shard_map/all_to_all | solution.py:126
  79.2 96.4 %reduce-scatter.2.cloned.1.call-start = ((), (), s32[]{:S(2)}) async-start(), calls=%async_computation.5 | async-start | bytes 3932160 | tf_op jit(solution)/shard_map/reduce_scatter | solution.py:136
  102.3 2.8 copy-start.5
  137.6 38.1 %copy-start.2 = (bf16[2048,192]{0,1:T(8,128)(2,1)S(1)}, bf16[2048,192]{0,1:T(8,128)(2,1)}, u32[]{:S(2)}) copy-start(bf16[2048,192]{0,1:T(8,128)(2,1)} %copy.34) | copy-start | bytes 2359300
  137.6 71.7 %copy-start.13 = (f32[768]{0:T(1024)S(1)}, f32[768]{0:T(1024)}, u32[]{:S(2)}) copy-start(f32[768]{0:T(1024)} %param.21) | copy-start | bytes 9220
  137.6 69.0 %all-gather.5.cloned.1.call-start = ((), (), s32[]{:S(2)}) async-start(), calls=%async_computation.6 | async-start | bytes 3932160 | tf_op jit(solution)/shard_map/all_gather | solution.py:142
  177.9 116.3 %all-reduce.3.cloned.1.call-start = ((), (), s32[]{:S(2)}) async-start(), calls=%async_computation.7 | async-start | bytes 884736 | tf_op jit(solution)/shard_map/psum | solution.py:179
  206.6 2.8 copy-start.1
  209.4 1.2 copy-start.10
  210.6 1.1 copy-start.3
  212.4 0.8 copy-start.14
  213.7 1.0 copy-start.8
  223.8 76.7 %copy-start.4 = (f32[1,2,192,384]{3,2,1,0:T(8,128)S(1)}, f32[1,2,192,384]{3,2,1,0:T(8,128)}, u32[]{:S(2)}) copy-start(f32[1,2,192,384]{3,2,1,0:T(8,128)} %param.24) | copy-start | bytes 1769476
  223.8 76.7 %copy-start.6 = (bf16[2048,192]{0,1:T(8,128)(2,1)S(1)}, bf16[2048,192]{0,1:T(8,128)(2,1)}, u32[]{:S(2)}) copy-start(bf16[2048,192]{0,1:T(8,128)(2,1)} %add_convert_fusion) | copy-start | bytes 2359300
  223.8 76.7 %copy-start.7 = (bf16[2048,192]{0,1:T(8,128)(2,1)S(1)}, bf16[2048,192]{0,1:T(8,128)(2,1)}, u32[]{:S(2)}) copy-start(bf16[2048,192]{0,1:T(8,128)(2,1)} %convolution_convert_fusion.5) | copy-start | bytes 2359300
  223.8 76.7 %copy-start.9 = (f32[1,384,192]{1,2,0:T(8,128)S(1)}, f32[1,384,192]{1,2,0:T(8,128)}, u32[]{:S(2)}) copy-start(f32[1,384,192]{1,2,0:T(8,128)} %param.25) | copy-start | bytes 884740
  294.2 6.3 %copy-start.11 = (bf16[192,384]{1,0:T(8,128)(2,1)S(1)}, bf16[192,384]{1,0:T(8,128)(2,1)}, u32[]{:S(2)}) copy-start(bf16[192,384]{1,0:T(8,128)(2,1)} %get-tuple-element.95) | copy-start | bytes 442372
  294.2 6.3 %copy-start.12 = (bf16[384,192]{0,1:T(8,128)(2,1)S(1)}, bf16[384,192]{0,1:T(8,128)(2,1)}, u32[]{:S(2)}) copy-start(bf16[384,192]{0,1:T(8,128)(2,1)} %get-tuple-element.96) | copy-start | bytes 442372
Sparse Core Ops, SparseCore 0:
  75.0 27.2 all-gather.2
  137.7 37.8 reduce-scatter.1
  178.1 28.4 all-gather.4
  221.3 72.8 all-reduce.2
where the time goes:
time: 312 us; the launch traced here: 311 us
  waiting for transfers between devices  190 us (61%)
  matrix products  50.9 us (16%)
  local copies, waits for them, and re-layouts  20.1 us (6%)
  other arithmetic  19.3 us (6%)
  starting transfers between devices  17.5 us (6%)
  between operations  13.5 us (4%)
    psum x1, waiting for transfers between devices, on_device(): lax.psum(grad_gate.astype(jnp.bfloat16), 'seq').astype(jnp.float32)  70.4 us
    reduce_scatter x1, waiting for transfers between devices, on_device(): lax.psum_scatter(partial_value.astype(jnp.bfloat16), 'head', scatter_dime...  38 us
    all_to_all x1, waiting for transfers between devices, on_device(): lax.all_to_all(pack_rows(selection, own_columns), 'seq', split_axis=0, co...  36.2 us
    all_gather x1, waiting for transfers between devices, on_device(): full_embedded = lax.all_gather(embedded, 'head', axis=1, tiled=True)  28.4 us
    sub x4, matrix products, attend_pair(): exp_scores = jnp.exp(scores - top_score)  11.9 us
    all_gather x1, waiting for transfers between devices, on_device(): lax.all_gather(view_own.reshape(BLK_DEV * BLK, width), 'head', axis=1, ti...  10.7 us
    dot_general x4, matrix products, attend_pair(): jnp.einsum('hqk,khe->qhe', weights, v_heads, preferred_element_type=jnp.f...  9.15 us
    all_to_all x1, starting transfers between devices, on_device(): lax.all_to_all(sent_dest, 'seq', split_axis=0, concat_axis=0, tiled=True)  7.28 us
  transfers between devices with their start and end apart: 7, of which 6 were waited for; matrix products, arithmetic and copies ran while one was open for 6% of the time, Pallas kernels for 0%

commit v1 on v0

--- a/solution.py
+++ b/solution.py
@@ -8,6 +8,12 @@
 BLK_DEV = 8
 EPSILON = 1e-06
 RATE_SCALE = 0.1
+
+
+def gather_and_add(shard, name):
+    blocks = lax.all_gather(shard, name, axis=0, tiled=False)
+    total = blocks.sum(axis=0)
+    return total
 
 
 def norm_rows(values, gain_vector):
@@ -176,7 +182,7 @@
     grad_gate = jnp.einsum("tf,th->fh", fast_key, gate_grad, preferred_element_type=jnp.float32)
     grad_up = jnp.einsum("tf,th->fh", fast_key, up_grad, preferred_element_type=jnp.float32)
     grad_gate, grad_up, grad_down = (
-        lax.psum(grad_gate.astype(jnp.bfloat16), "seq").astype(jnp.float32),
+        gather_and_add(grad_gate.astype(jnp.bfloat16), "seq").astype(jnp.float32),
         lax.psum(grad_up.astype(jnp.bfloat16), "seq").astype(jnp.float32),
         lax.psum(grad_down.astype(jnp.bfloat16), "seq").astype(jnp.float32),
     )

time: 312 us -> 351 us (1.12)
  waiting for transfers between devices: 190 us -> 223 us
  matrix products: 50.9 us -> 54.5 us
    all_gather x0 -> x1, waiting for transfers between devices: none -> 41.1 us  [gather_and_add(): blocks = lax.all_gather(shard, name, axis=0, tiled=False)]
    psum x1, waiting for transfers between devices: 70.4 us -> 62.8 us  [on_device(): lax.psum(grad_up.astype(jnp.bfloat16), 'seq').astype(jnp.float32)]
    dot_general x1, matrix products: 2.13 us -> 6.09 us  [on_device(): jnp.einsum('tf,th->fh', fast_key, gate_grad, preferred_element_type=jnp.f...]
  transfers between devices with their start and end apart: 7 -> 8, of which waited for: 6 -> 7; matrix products, arithmetic and copies ran while one was open for 6% -> 7% of each run, Pallas kernels for 0% -> 0%
where the time goes in v1:
time: 351 us; the launch traced here: 350 us
  waiting for transfers between devices  223 us (64%)
  matrix products  54.5 us (16%)
  other arithmetic  20.8 us (6%)
  local copies, waits for them, and re-layouts  20.3 us (6%)
  starting transfers between devices  17.5 us (5%)
  between operations  13.6 us (4%)
    psum x1, waiting for transfers between devices, on_device(): lax.psum(grad_up.astype(jnp.bfloat16), 'seq').astype(jnp.float32)  62.8 us
    all_gather x1, waiting for transfers between devices, gather_and_add(): blocks = lax.all_gather(shard, name, axis=0, tiled=False)  41.1 us
    reduce_scatter x1, waiting for transfers between devices, on_device(): lax.psum_scatter(partial_value.astype(jnp.bfloat16), 'head', scatter_dime...  38 us
    all_to_all x1, waiting for transfers between devices, on_device(): lax.all_to_all(pack_rows(selection, own_columns), 'seq', split_axis=0, co...  36.2 us
    all_gather x1, waiting for transfers between devices, on_device(): full_embedded = lax.all_gather(embedded, 'head', axis=1, tiled=True)  28.4 us
    sub x4, matrix products, attend_pair(): exp_scores = jnp.exp(scores - top_score)  11.8 us
    all_gather x1, waiting for transfers between devices, on_device(): lax.all_gather(view_own.reshape(BLK_DEV * BLK, width), 'head', axis=1, ti...  10.7 us
    dot_general x4, matrix products, attend_pair(): jnp.einsum('hqk,khe->qhe', weights, v_heads, preferred_element_type=jnp.f...  9.14 us
  transfers between devices with their start and end apart: 8, of which 7 were waited for; matrix products, arithmetic and copies ran while one was open for 7% of the time, Pallas kernels for 0%

profile of v1, /device:TPU:0, one launch (start us, length us, event | category | flops | bytes accessed | tf_op | source)
XLA Modules:
  0.0 350.4 jit_solution(12756844559185382576)
XLA Ops:
  9.6 7.3 %all-to-all-start = ((s32[8,2,1]{1,2,0:T(1,128)}), s32[8,2,1]{1,2,0:T(1,128)S(1)}, u32[]{:S(2)}, u32[]{:S(2)}) async-start(s32[8,2,1]{1,2,0:T(1,128)} %bitcast.6), calls=%async_computation | async-start | bytes 8192 | tf_op jit(solution)/shard_map/all_to_all | solution.py:131
  16.8 2.9 constant_dynamic-slice_fusion.4
  19.8 3.2 reshape.274
  23.0 2.0 convolution_convert_fusion
  26.9 6.0 %all-to-all-start.1 = ((bf16[8,2,49152]{2,1,0:T(2,128)(2,1)}), bf16[8,2,49152]{2,1,0:T(2,128)(2,1)S(1)}, u32[]{:S(2)}, u32[]{:S(2)}) async-start(bf16[8,2,49152]{2,1,0:T(2,128)(2,1)} %all_to_all.17), calls=%async_computation.1 | async-start | bytes 3145728 | tf_op jit(solution)/shard_map/all_to_all | solution.py:128
  33.1 36.2 %all-to-all-done.1 = bf16[8,2,49152]{2,1,0:T(2,128)(2,1)S(1)} async-done(((bf16[8,2,49152]{2,1,0:T(2,128)(2,1)}), bf16[8,2,49152]{2,1,0:T(2,128)(2,1)S(1)}, u32[]{:S(2)}, u32[]{:S(2)}) %all-to-all-start.1) | async-done | bytes 1572896 | tf_op jit(solution)/shard_map/all_to_all | solution.py:128
  71.3 2.3 reshape.275
  75.5 3.6 %all-to-all-start.2 = ((s32[8,2,1]{1,2,0:T(1,128)}), s32[8,2,1]{1,2,0:T(1,128)S(1)}, u32[]{:S(2)}, u32[]{:S(2)}) async-start(s32[8,2,1]{1,2,0:T(1,128)} %bitcast.9), calls=%async_computation.2 | async-start | bytes 8192 | tf_op jit(solution)/shard_map/all_to_all | solution.py:132
  79.4 6.3 %all-to-all-done.2 = s32[8,2,1]{1,2,0:T(1,128)S(1)} async-done(((s32[8,2,1]{1,2,0:T(1,128)}), s32[8,2,1]{1,2,0:T(1,128)S(1)}, u32[]{:S(2)}, u32[]{:S(2)}) %all-to-all-start.2) | async-done | bytes 96 | tf_op jit(solution)/shard_map/all_to_all | solution.py:132
  86.6 5.0 %select_select_fusion = s32[2048]{0:T(1024)S(1)} fusion(pred[2048]{0:T(1024)(128)(4,1)S(1)} %copy-done.25, pred[2048]{0:T(1024)(128)(4,1)S(1)} %copy-done.24, pred[2048]{0:T(1024)(128)(4,1)S(1)} %copy-done.23, pred[2048]{0:T(1024)(128)(4,1)S(1)} %copy-done.22, pred[2048]{0:T(1024)(128)(4,1)S(1)} %copy-done.21, pred[2048]{0:T(1024)(128)(4,1)S(1)} %copy-done.20, ...), kind=kLoop, calls=%fused_computation.103 | loop fusion | flops 14336 | bytes 22560 | tf_op jit(solution)/shard_map/jit(_take)/gather | solution.py:52
  91.6 10.7 %all-gather.5.cloned.1.call-done = bf16[2048,768]{0,1:T(8,128)(2,1)} async-done(((bf16[2048,192]{0,1:T(8,128)(2,1)}), bf16[2048,768]{0,1:T(8,128)(2,1)}) %all-gather.5.cloned.1.call-update) | async-done | bytes 3145744 | tf_op jit(solution)/shard_map/all_gather | solution.py:139
  102.3 2.7 fusion.11
  108.6 25.0 %while.11 = (s32[]{:T(128)}, bf16[4,512,192]{1,2,0:T(8,128)(2,1)}, bf16[4,512,192]{1,2,0:T(8,128)(2,1)S(1)}, s32[4,512]{1,0:T(4,128)S(1)}, bf16[4,512,192]{1,2,0...) while((s32[]{:T(128)}, bf16[4,512,192]{1,2,0:T(8,128)(2,1)}, ...), condition=%wide.region_8.9_spmd, body=%wide.region_5.8_spmd.sunk | while | flops 206406144 | bytes 9193573 | solution.py:55
  108.9 3.0 fusion.111
  111.9 2.3 fusion.112
  115.2 3.0 fusion.111
  118.2 2.3 fusion.112
  121.5 3.0 fusion.111
  124.4 2.3 fusion.112
  127.7 3.0 fusion.111
  130.6 2.3 fusion.112
  134.9 2.7 convolution_convert_fusion.2
  137.6 38.0 %reduce-scatter.2.cloned.1.call-done = bf16[2048,192]{0,1:T(8,128)(2,1)} async-done(((bf16[2048,768]{0,1:T(8,128)(2,1)}), bf16[2048,192]{0,1:T(8,128)(2,1)}) %reduce-scatter.2.cloned.1.call-update) | async-done | bytes 786448 | tf_op jit(solution)/shard_map/reduce_scatter | solution.py:142
  175.6 2.3 add_convert_fusion
  178.2 28.4 %all-gather.7.cloned.1.call-done = bf16[2048,768]{0,1:T(8,128)(2,1)} async-done(((bf16[2048,192]{0,1:T(8,128)(2,1)}), bf16[2048,768]{0,1:T(8,128)(2,1)}) %all-gather.7.cloned.1.call-update) | async-done | bytes 3145744 | tf_op jit(solution)/shard_map/all_gather | solution.py:148
  206.6 2.7 fusion.14
  219.4 6.1 %fusion.27 = bf16[192,384]{1,0:T(8,128)(2,1)} fusion(bf16[2048,192]{0,1:T(8,128)(2,1)} %copy-done.2, f32[2048,384]{1,0:T(8,128)} %copy-done.7, f32[2048,384]{1,0:T(8,128)} %copy-done.9, f32[2048,384]{1,0:T(8,128)} %copy-done.8), kind=kOutput, calls=%fused_computation.55 | convolution fusion | flops 309927936 | bytes 10371072 | tf_op jit(solution)/shard_map/tf,th->fh/dot_general | solution.py:182
  225.5 2.7 convolution_convert_fusion.5
  228.2 62.8 %all-reduce.3.cloned.1.call-done = (bf16[192,384]{1,0:T(8,128)(2,1)}, bf16[384,192]{0,1:T(8,128)(2,1)}) async-done(((bf16[192,384]{1,0:T(8,128)(2,1)}, bf16[384,192]{0,1:T(8,128)(2,1)}), (bf16[192,384]{1,0:T(8,128)(2,1)}, bf16[384,192]{0,1:T(8,128)(2,1)})) %all-reduce.3.cloned.1.call-update) | async-done | bytes 294928 | tf_op jit(solution)/shard_map/psum | solution.py:186
  292.0 41.1 %all-gather.9.cloned.1.call-done = bf16[1536,384]{1,0:T(8,128)(2,1)} async-done(((bf16[192,384]{1,0:T(8,128)(2,1)}), bf16[1536,384]{1,0:T(8,128)(2,1)}) %all-gather.9.cloned.1.call-update) | async-done | bytes 1179664 | tf_op jit(solution)/shard_map/all_gather | solution.py:14
  336.1 3.4 fusion.45
  339.6 4.3 %fusion.18 = bf16[2048,192]{0,1:T(8,128)(2,1)} fusion(bf16[2048,192]{0,1:T(8,128)(2,1)S(1)} %copy-done.10, f32[2048,384]{1,0:T(8,128)} %fusion.45, bf16[2048,192]{0,1:T(8,128)(2,1)S(1)} %copy-done.11, bf16[192,384]{1,0:T(8,128)(2,1)S(1)} %copy-done.15, f32[1,2,192,384]{3,2,1,0:T(8,128)S(1)} %copy-done.5, bf16[384,192]{0,1:T(8,128)(2,1)S(1)} %copy-done.16, ...), kind=kOutput, calls=%fused_computation.39 | convolution fusion | flops 610615296 | bytes 6395904 | tf_op jit(solution)/shard_map/dot_general | solution.py:198
  (138 shorter events, 33.2 us)
Async XLA Ops:
  6.5 128.3 %copy-start = (bf16[192,768]{1,0:T(8,128)(2,1)S(1)}, bf16[192,768]{1,0:T(8,128)(2,1)}, u32[]{:S(2)}) copy-start(bf16[192,768]{1,0:T(8,128)(2,1)} %param.20) | copy-start | bytes 884740
  9.6 17.3 %all-to-all-start = ((s32[8,2,1]{1,2,0:T(1,128)}), s32[8,2,1]{1,2,0:T(1,128)S(1)}, u32[]{:S(2)}, u32[]{:S(2)}) async-start(s32[8,2,1]{1,2,0:T(1,128)} %bitcast.6), calls=%async_computation | async-start | bytes 8192 | tf_op jit(solution)/shard_map/all_to_all | solution.py:131
  26.9 42.4 %all-to-all-start.1 = ((bf16[8,2,49152]{2,1,0:T(2,128)(2,1)}), bf16[8,2,49152]{2,1,0:T(2,128)(2,1)S(1)}, u32[]{:S(2)}, u32[]{:S(2)}) async-start(bf16[8,2,49152]{2,1,0:T(2,128)(2,1)} %all_to_all.17), calls=%async_computation.1 | async-start | bytes 3145728 | tf_op jit(solution)/shard_map/all_to_all | solution.py:128
  32.9 69.4 %all-gather.5.cloned.1.call-start = ((), (), s32[]{:S(2)}) async-start(), calls=%async_computation.4 | async-start | bytes 3932160 | tf_op jit(solution)/shard_map/all_gather | solution.py:139
  69.9 16.6 %copy-start.19 = (pred[2048]{0:T(1024)(128)(4,1)S(1)}, pred[2048]{0:T(1024)(128)(4,1)}, u32[]{:S(2)}) copy-start(pred[2048]{0:T(1024)(128)(4,1)} %constant.201) | copy-start | bytes 6148
  69.9 16.6 %copy-start.20 = (pred[2048]{0:T(1024)(128)(4,1)S(1)}, pred[2048]{0:T(1024)(128)(4,1)}, u32[]{:S(2)}) copy-start(pred[2048]{0:T(1024)(128)(4,1)} %constant.200) | copy-start | bytes 6148
  70.0 16.6 %copy-start.21 = (pred[2048]{0:T(1024)(128)(4,1)S(1)}, pred[2048]{0:T(1024)(128)(4,1)}, u32[]{:S(2)}) copy-start(pred[2048]{0:T(1024)(128)(4,1)} %constant.199) | copy-start | bytes 6148
  70.0 16.6 %copy-start.22 = (pred[2048]{0:T(1024)(128)(4,1)S(1)}, pred[2048]{0:T(1024)(128)(4,1)}, u32[]{:S(2)}) copy-start(pred[2048]{0:T(1024)(128)(4,1)} %constant.198) | copy-start | bytes 6148
  70.0 16.6 %copy-start.23 = (pred[2048]{0:T(1024)(128)(4,1)S(1)}, pred[2048]{0:T(1024)(128)(4,1)}, u32[]{:S(2)}) copy-start(pred[2048]{0:T(1024)(128)(4,1)} %constant.197) | copy-start | bytes 6148
  70.0 16.6 %copy-start.24 = (pred[2048]{0:T(1024)(128)(4,1)S(1)}, pred[2048]{0:T(1024)(128)(4,1)}, u32[]{:S(2)}) copy-start(pred[2048]{0:T(1024)(128)(4,1)} %constant.196) | copy-start | bytes 6148
  70.0 16.6 %copy-start.25 = (pred[2048]{0:T(1024)(128)(4,1)S(1)}, pred[2048]{0:T(1024)(128)(4,1)}, u32[]{:S(2)}) copy-start(pred[2048]{0:T(1024)(128)(4,1)} %constant.195) | copy-start | bytes 6148
  73.6 31.4 %copy-start.26 = (bf16[3,768,192]{1,2,0:T(8,128)(2,1)S(1)}, bf16[3,768,192]{1,2,0:T(8,128)(2,1)}, u32[]{:S(2)}) copy-start(bf16[3,768,192]{1,2,0:T(8,128)(2,1)} %param.19) | copy-start | bytes 2654212
  73.6 31.4 %copy-start.27 = (f32[768]{0:T(1024)S(1)}, f32[768]{0:T(1024)}, u32[]{:S(2)}) copy-start(f32[768]{0:T(1024)} %param.18) | copy-start | bytes 9220
  75.5 10.1 %all-to-all-start.2 = ((s32[8,2,1]{1,2,0:T(1,128)}), s32[8,2,1]{1,2,0:T(1,128)S(1)}, u32[]{:S(2)}, u32[]{:S(2)}) async-start(s32[8,2,1]{1,2,0:T(1,128)} %bitcast.9), calls=%async_computation.2 | async-start | bytes 8192 | tf_op jit(solution)/shard_map/all_to_all | solution.py:132
  79.2 96.4 %reduce-scatter.2.cloned.1.call-start = ((), (), s32[]{:S(2)}) async-start(), calls=%async_computation.5 | async-start | bytes 3932160 | tf_op jit(solution)/shard_map/reduce_scatter | solution.py:142
  102.3 2.8 copy-start.6
  137.6 38.1 %copy-start.3 = (bf16[2048,192]{0,1:T(8,128)(2,1)S(1)}, bf16[2048,192]{0,1:T(8,128)(2,1)}, u32[]{:S(2)}) copy-start(bf16[2048,192]{0,1:T(8,128)(2,1)} %copy.34) | copy-start | bytes 2359300
  137.6 71.7 %copy-start.17 = (f32[768]{0:T(1024)S(1)}, f32[768]{0:T(1024)}, u32[]{:S(2)}) copy-start(f32[768]{0:T(1024)} %param.21) | copy-start | bytes 9220
  137.6 69.0 %all-gather.7.cloned.1.call-start = ((), (), s32[]{:S(2)}) async-start(), calls=%async_computation.6 | async-start | bytes 3932160 | tf_op jit(solution)/shard_map/all_gather | solution.py:148
  177.9 113.0 %all-reduce.3.cloned.1.call-start = ((), (), s32[]{:S(2)}) async-start(), calls=%async_computation.8 | async-start | bytes 589824 | tf_op jit(solution)/shard_map/psum | solution.py:186
  206.6 2.8 copy-start.1
  211.7 5.8 %copy-start.2 = (bf16[2048,192]{0,1:T(8,128)(2,1)}, bf16[2048,192]{0,1:T(8,128)(2,1)S(1)}, u32[]{:S(2)}) copy-start(bf16[2048,192]{0,1:T(8,128)(2,1)S(1)} %convolution_convert_fusion.4) | copy-start | bytes 2359300
  212.4 5.1 %copy-start.7 = (f32[2048,384]{1,0:T(8,128)}, f32[2048,384]{1,0:T(8,128)S(1)}, u32[]{:S(2)}) copy-start(f32[2048,384]{1,0:T(8,128)S(1)} %fusion.46) | copy-start | bytes 9437188
  213.2 2.5 copy-start.8
  215.7 1.8 copy-start.9
  219.3 113.8 %all-gather.9.cloned.1.call-start = ((), (), s32[]{:S(2)}) async-start(), calls=%async_computation.7 | async-start | bytes 1327104 | tf_op jit(solution)/shard_map/all_gather | solution.py:14
  228.2 108.0 %copy-start.11 = (bf16[2048,192]{0,1:T(8,128)(2,1)S(1)}, bf16[2048,192]{0,1:T(8,128)(2,1)}, u32[]{:S(2)}) copy-start(bf16[2048,192]{0,1:T(8,128)(2,1)} %convolution_convert_fusion.5) | copy-start | bytes 2359300
  333.2 6.4 %copy-start.5 = (f32[1,2,192,384]{3,2,1,0:T(8,128)S(1)}, f32[1,2,192,384]{3,2,1,0:T(8,128)}, u32[]{:S(2)}) copy-start(f32[1,2,192,384]{3,2,1,0:T(8,128)} %param.24) | copy-start | bytes 1769476
  333.2 6.4 %copy-start.10 = (bf16[2048,192]{0,1:T(8,128)(2,1)S(1)}, bf16[2048,192]{0,1:T(8,128)(2,1)}, u32[]{:S(2)}) copy-start(bf16[2048,192]{0,1:T(8,128)(2,1)} %add_convert_fusion) | copy-start | bytes 2359300
  333.2 6.4 %copy-start.13 = (f32[1,384,192]{1,2,0:T(8,128)S(1)}, f32[1,384,192]{1,2,0:T(8,128)}, u32[]{:S(2)}) copy-start(f32[1,384,192]{1,2,0:T(8,128)} %param.25) | copy-start | bytes 884740
  333.2 6.4 %copy-start.15 = (bf16[192,384]{1,0:T(8,128)(2,1)S(1)}, bf16[192,384]{1,0:T(8,128)(2,1)}, u32[]{:S(2)}) copy-start(bf16[192,384]{1,0:T(8,128)(2,1)} %get-tuple-element.94) | copy-start | bytes 442372
  333.2 6.4 %copy-start.16 = (bf16[384,192]{0,1:T(8,128)(2,1)S(1)}, bf16[384,192]{0,1:T(8,128)(2,1)}, u32[]{:S(2)}) copy-start(bf16[384,192]{0,1:T(8,128)(2,1)} %get-tuple-element.95) | copy-start | bytes 442372
  (4 other events, 4.2 us)
Sparse Core Ops, SparseCore 0:
  75.0 27.2 all-gather.4
  137.7 37.8 reduce-scatter.1
  178.1 28.4 all-gather.6
  219.4 71.4 all-reduce.2
  292.9 40.1 all-gather.8
